TPU v7x, 32 devices: a whole 2x2x4 slice. The times are simulated.
32 devices in a mesh: dp: 4 (over y, core), seq: 8 (over z, x).
Axes of the slice: x: 2, y: 2, z: 4, core: 2. Of those that a mesh axis runs over, the one named last changes fastest.
Arguments:
- queries: bfloat16 [32, 2048, 512], P('dp', 'seq'), may hold values from -6 to 6
- enc_keys: bfloat16 [32, 2048, 512], P('dp', 'seq'), may hold values from -6 to 6
- enc_values: bfloat16 [32, 2048, 512], P('dp', 'seq'), may hold values from -6 to 6
- dec_ids: int32 [32, 2048], P('dp', 'seq'), may hold values from 0 to 15, never falling along the last dimension, each value on 1 to 512 neighbouring positions
- enc_ids: int32 [32, 2048], P('dp', 'seq'), may hold values from 0 to 15, never falling along the last dimension, each value on 1 to 512 neighbouring positions
Outputs:
- context: bfloat16 [32, 2048, 512], P('dp', 'seq')
Inputs may be any that keep to these rules, and one draw needn't show every extreme that they name: `dec_ids`: along each row the numbers never fall; every number from 0 to 15 occurs in every row; a document holds 1 to 512 positions of a row, and some document holds exactly 512. `enc_ids`: along each row the numbers never fall; every number from 0 to 15 occurs in every row; a document holds 1 to 512 positions of a row, and some document holds exactly 512.
All inputs are finite; a program needn't handle non-finite values.
Results may differ from a plain program's by a relative error of at most 0.0047.
Values may be sent and summed in bfloat16 or wider, within the bound.
No kernel may reach another device: no remote copies, remote signals or barrier semaphores. Data moves between devices by JAX's collectives and lax.ppermute only.
A program may use at most 128 MiB of HBM per device.

v0:
```python
import jax
import jax.numpy as jnp
from jax import lax
from jax.sharding import PartitionSpec as P

HEAD_DIM = 64
masked_score = -1e30


def shortened(value):

    def short(part):
        return part.astype(jnp.bfloat16) if part.dtype == jnp.float32 else part

    return jax.tree.map(short, value)


def attend_dense(query_row, key_row, value_row, dec_row, enc_row, head_count):
    length = query_row.shape[0]
    query_heads = query_row.reshape(length, head_count, HEAD_DIM)
    key_heads = key_row.reshape(length, head_count, HEAD_DIM)
    value_heads = value_row.reshape(length, head_count, HEAD_DIM)
    query_span = min(512, length)
    pieces = []
    for offset in range(0, length, query_span):
        scores = jnp.einsum(
            "qhd,khd->hqk",
            query_heads[offset : offset + query_span],
            key_heads,
            preferred_element_type=jnp.float32,
        )
        allowed = (dec_row[offset : offset + query_span][:, None] == enc_row[None, :])[None]
        scores = jnp.where(allowed, scores, masked_score)
        row_peak = jnp.max(scores, axis=2, keepdims=True)
        expos = jnp.where(allowed, jnp.exp(scores - row_peak), 0.0)
        row_total = jnp.sum(expos, axis=2, keepdims=True)
        weights = (expos / row_total).astype(jnp.bfloat16)
        summed = jnp.einsum(
            "hqk,khd->qhd", weights, value_heads, preferred_element_type=jnp.float32
        )
        pieces.append(summed.reshape(query_span, head_count * HEAD_DIM).astype(jnp.bfloat16))
    return jnp.concatenate(pieces, axis=0)


def local(queries, enc_keys, enc_values, dec_ids, enc_ids):
    group = lax.axis_size("seq")
    dec_spread = jnp.broadcast_to(
        dec_ids.astype(jnp.bfloat16)[:, :, None], (dec_ids.shape[0], dec_ids.shape[1], group)
    )
    enc_spread = jnp.broadcast_to(
        enc_ids.astype(jnp.bfloat16)[:, :, None], (enc_ids.shape[0], enc_ids.shape[1], group)
    )
    members = (
        lax.all_to_all(queries, "seq", split_axis=2, concat_axis=1, tiled=True),
        lax.all_to_all(enc_keys, "seq", split_axis=2, concat_axis=1, tiled=True),
        lax.all_to_all(enc_values, "seq", split_axis=2, concat_axis=1, tiled=True),
        lax.all_to_all(dec_spread, "seq", split_axis=2, concat_axis=1, tiled=True),
        lax.all_to_all(enc_spread, "seq", split_axis=2, concat_axis=1, tiled=True),
    )
    dec_rows = members[3][:, :, 0].astype(jnp.int32)
    enc_rows = members[4][:, :, 0].astype(jnp.int32)
    query_rows = members[0]
    key_rows = members[1]
    value_rows = members[2]
    head_count = query_rows.shape[2] // HEAD_DIM

    def one_row(members):
        return attend_dense(members[0], members[1], members[2], members[3], members[4], head_count)

    attended = lax.map(one_row, (query_rows, key_rows, value_rows, dec_rows, enc_rows))
    return lax.all_to_all(
        shortened(attended), "seq", split_axis=1, concat_axis=2, tiled=True
    ).astype(attended.dtype)


def solution(mesh):
    in_specs = (
        P("dp", "seq", None),
        P("dp", "seq", None),
        P("dp", "seq", None),
        P("dp", "seq"),
        P("dp", "seq"),
    )
    out_specs = P("dp", "seq", None)
    return jax.shard_map(local, mesh=mesh, in_specs=in_specs, out_specs=out_specs, check_vma=False)
```

profile of v0, /device:TPU:0, one launch (start us, length us, event | category | flops | bytes accessed | tf_op | source)
XLA Modules:
  0.0 412.9 jit_solution(16733577638339409978)
XLA Ops:
  1.3 7.3 %all-to-all-start.1 = ((bf16[8,256,8]{1,0,2:T(8,128)(2,1)}), bf16[8,256,8]{1,0,2:T(8,128)(2,1)S(1)}, u32[]{:S(2)}, u32[]{:S(2)}) async-start(bf16[8,256,8]{1,0,2:T(8,128)(2,1)} %broadcast_in_dim.23), calls=%async_computation.1 | async-start | bytes 65536 | tf_op jit(solution)/shard_map/all_to_all | solution.py:57
  9.3 6.0 %all-to-all-done.1 = bf16[8,256,8]{1,0,2:T(8,128)(2,1)S(1)} async-done(((bf16[8,256,8]{1,0,2:T(8,128)(2,1)}), bf16[8,256,8]{1,0,2:T(8,128)(2,1)S(1)}, u32[]{:S(2)}, u32[]{:S(2)}) %all-to-all-start.1) | async-done | bytes 32800 | tf_op jit(solution)/shard_map/all_to_all | solution.py:57
  19.2 4.5 %copy.25 = bf16[8,256,512]{1,0,2:T(8,128)(2,1)} copy(bf16[8,256,512]{2,1,0:T(8,128)(2,1)} %param.9) | data formatting | bytes 4194304 | tf_op args[2]
  25.9 3.8 all-to-all-start
  29.7 4.5 %copy.28 = bf16[8,256,512]{1,0,2:T(8,128)(2,1)} copy(bf16[8,256,512]{2,1,0:T(8,128)(2,1)} %param.7) | data formatting | bytes 4194304 | tf_op args[0]
  34.2 42.1 %all-to-all-done = bf16[8,256,512]{1,0,2:T(8,128)(2,1)S(1)} async-done(((bf16[8,256,512]{1,0,2:T(8,128)(2,1)}), bf16[8,256,512]{1,0,2:T(8,128)(2,1)S(1)}, u32[]{:S(2)}, u32[]{:S(2)}) %all-to-all-start) | async-done | bytes 2097184 | tf_op jit(solution)/shard_map/all_to_all | solution.py:56
  76.3 4.4 %all-to-all-start.3 = ((bf16[8,256,512]{1,0,2:T(8,128)(2,1)}), bf16[8,256,512]{1,0,2:T(8,128)(2,1)}, u32[]{:S(2)}, u32[]{:S(2)}) async-start(bf16[8,256,512]{1,0,2:T(8,128)(2,1)} %copy.28), calls=%async_computation.3 | async-start | bytes 4194304 | tf_op jit(solution)/shard_map/all_to_all | solution.py:54
  80.7 4.5 %copy.31 = bf16[8,256,512]{1,0,2:T(8,128)(2,1)} copy(bf16[8,256,512]{2,1,0:T(8,128)(2,1)} %param.8) | data formatting | bytes 4194304 | tf_op args[1]
  85.2 43.1 %all-to-all-done.3 = bf16[8,256,512]{1,0,2:T(8,128)(2,1)} async-done(((bf16[8,256,512]{1,0,2:T(8,128)(2,1)}), bf16[8,256,512]{1,0,2:T(8,128)(2,1)}, u32[]{:S(2)}, u32[]{:S(2)}) %all-to-all-start.3) | async-done | bytes 2097184 | tf_op jit(solution)/shard_map/all_to_all | solution.py:54
  128.3 4.4 %all-to-all-start.4 = ((bf16[8,256,512]{1,0,2:T(8,128)(2,1)}), bf16[8,256,512]{1,0,2:T(8,128)(2,1)}, u32[]{:S(2)}, u32[]{:S(2)}) async-start(bf16[8,256,512]{1,0,2:T(8,128)(2,1)} %copy.31), calls=%async_computation.4 | async-start | bytes 4194304 | tf_op jit(solution)/shard_map/all_to_all | solution.py:55
  132.7 3.5 copy.42
  136.3 5.0 %copy.44 = bf16[8,8,256,64]{3,2,1,0:T(8,128)(2,1)} copy(bf16[8,8,256,64]{2,0,3,1:T(8,128)(2,1)} %bitcast.36) | data formatting | bytes 4194304 | tf_op jit(solution)/shard_map/while | solution.py:70
  141.3 39.2 %all-to-all-done.4 = bf16[8,256,512]{1,0,2:T(8,128)(2,1)} async-done(((bf16[8,256,512]{1,0,2:T(8,128)(2,1)}), bf16[8,256,512]{1,0,2:T(8,128)(2,1)}, u32[]{:S(2)}, u32[]{:S(2)}) %all-to-all-start.4) | async-done | bytes 2097184 | tf_op jit(solution)/shard_map/all_to_all | solution.py:55
  180.5 5.0 %copy.46 = bf16[8,8,256,64]{3,2,1,0:T(8,128)(2,1)} copy(bf16[8,8,256,64]{2,0,3,1:T(8,128)(2,1)} %bitcast.40) | data formatting | bytes 4194304 | tf_op jit(solution)/shard_map/while | solution.py:70
  185.5 150.7 %while.10 = (s32[]{:T(128)}, bf16[8,2048,64]{1,2,0:T(8,128)(2,1)S(1)}, bf16[8,2048,64]{2,1,0:T(8,128)(2,1)}, s32[8,2048]{1,0:T(8,128)S(1)}, s32[8,2048]{1,0:T(8,...) while((s32[]{:T(128)}, ...), condition=%wide.region_9.10_spmd, body=%wide.region_0.9_spmd.sunk | while | flops 1133637632 | bytes 72773864 | solution.py:70
  191.2 3.9 fusion.85
  210.1 3.9 fusion.85
  215.4 3.4 fusion.86
  228.9 3.9 fusion.85
  234.2 3.4 fusion.86
  247.7 3.9 fusion.85
  253.0 3.4 fusion.86
  266.6 3.9 fusion.85
  285.4 3.9 fusion.85
  290.7 3.4 fusion.86
  304.2 3.9 fusion.85
  323.1 3.9 fusion.85
  336.2 4.3 %copy.37 = bf16[8,2048,64]{2,0,1:T(8,128)(2,1)} copy(bf16[8,2048,64]{1,2,0:T(8,128)(2,1)S(1)} %get-tuple-element.42) | data formatting | bytes 4194304 | tf_op jit(solution)/shard_map/while | solution.py:70
  340.5 6.4 %reshape.166 = bf16[8,2,65536]{2,1,0:T(2,128)(2,1)S(1)} reshape(bf16[2048,8,64]{2,1,0:T(8,128)(2,1)} %bitcast.147) | data formatting | bytes 4194304
  346.8 51.8 %all_to_all.90 = bf16[8,2,65536]{2,1,0:T(2,128)(2,1)} all-to-all(bf16[8,2,65536]{2,1,0:T(2,128)(2,1)S(1)} %reshape.166), channel_id=1, replica_groups=mesh['dp'=4,'seq'=8] {'seq'}, dimensions={0} | all-to-all | bytes 4194304 | tf_op jit(solution)/shard_map/all_to_all | solution.py:71
  398.7 7.4 %reshape.167 = bf16[2048,8,64]{2,1,0:T(8,128)(2,1)} reshape(bf16[8,2,65536]{2,1,0:T(2,128)(2,1)} %all_to_all.90) | data formatting | bytes 4194304
  406.1 4.5 %copy.39 = bf16[8,256,8,64]{1,3,2,0:T(8,128)(2,1)S(1)} copy(bf16[8,256,8,64]{3,0,1,2:T(8,128)(2,1)} %bitcast.148) | data formatting | bytes 4194304 | tf_op jit(solution)/shard_map/all_to_all | solution.py:71
  (112 shorter events, 115.9 us)
Async XLA Ops:
  1.3 14.0 %all-to-all-start.1 = ((bf16[8,256,8]{1,0,2:T(8,128)(2,1)}), bf16[8,256,8]{1,0,2:T(8,128)(2,1)S(1)}, u32[]{:S(2)}, u32[]{:S(2)}) async-start(bf16[8,256,8]{1,0,2:T(8,128)(2,1)} %broadcast_in_dim.23), calls=%async_computation.1 | async-start | bytes 65536 | tf_op jit(solution)/shard_map/all_to_all | solution.py:57
  15.9 10.0 %all-to-all-start.2 = ((bf16[8,256,8]{1,0,2:T(8,128)(2,1)}), bf16[8,256,8]{1,0,2:T(8,128)(2,1)S(1)}, u32[]{:S(2)}, u32[]{:S(2)}) async-start(bf16[8,256,8]{1,0,2:T(8,128)(2,1)} %broadcast_in_dim.24), calls=%async_computation.2 | async-start | bytes 65536 | tf_op jit(solution)/shard_map/all_to_all | solution.py:58
  25.9 50.4 %all-to-all-start = ((bf16[8,256,512]{1,0,2:T(8,128)(2,1)}), bf16[8,256,512]{1,0,2:T(8,128)(2,1)S(1)}, u32[]{:S(2)}, u32[]{:S(2)}) async-start(bf16[8,256,512]{1,0,2:T(8,128)(2,1)} %copy.25), calls=%async_computation | async-start | bytes 4194304 | tf_op jit(solution)/shard_map/all_to_all | solution.py:56
  76.3 52.0 %all-to-all-start.3 = ((bf16[8,256,512]{1,0,2:T(8,128)(2,1)}), bf16[8,256,512]{1,0,2:T(8,128)(2,1)}, u32[]{:S(2)}, u32[]{:S(2)}) async-start(bf16[8,256,512]{1,0,2:T(8,128)(2,1)} %copy.28), calls=%async_computation.3 | async-start | bytes 4194304 | tf_op jit(solution)/shard_map/all_to_all | solution.py:54
  128.3 52.2 %all-to-all-start.4 = ((bf16[8,256,512]{1,0,2:T(8,128)(2,1)}), bf16[8,256,512]{1,0,2:T(8,128)(2,1)}, u32[]{:S(2)}, u32[]{:S(2)}) async-start(bf16[8,256,512]{1,0,2:T(8,128)(2,1)} %copy.31), calls=%async_computation.4 | async-start | bytes 4194304 | tf_op jit(solution)/shard_map/all_to_all | solution.py:55
  141.3 44.2 %copy-start.1 = (bf16[8,2048,64]{1,2,0:T(8,128)(2,1)S(1)}, bf16[8,2048,64]{1,2,0:T(8,128)(2,1)}, u32[]{:S(2)}) copy-start(bf16[8,2048,64]{1,2,0:T(8,128)(2,1)} %custom-call) | copy-start | bytes 6291460
  191.2 3.9 copy-start
  210.0 3.9 copy-start
  228.9 3.9 copy-start
  247.7 3.9 copy-start
  266.6 3.9 copy-start
  285.4 3.9 copy-start
  304.2 3.9 copy-start
  323.1 3.9 copy-start
where the time goes:
time: 415 us; the launch traced here: 413 us
  waiting for transfers between devices  133 us (32%)
  matrix products  122 us (29%)
  local copies, waits for them, and re-layouts  54 us (13%)
  blocking collectives  51.8 us (12%)
  other arithmetic  29 us (7%)
  starting transfers between devices  23.1 us (6%)
    dot_general x32, matrix products, attend_dense(): jnp.einsum('qhd,khd->hqk', query_heads[offset:offset + query_span], key_h...  75.9 us
    all_to_all x1, blocking collectives, local(): lax.all_to_all(shortened(attended), 'seq', split_axis=1, concat_axis=2, t...  51.8 us
    dot_general x32, matrix products, attend_dense(): jnp.einsum('hqk,khd->qhd', weights, value_heads, preferred_element_type=j...  45.9 us
    all_to_all x1, waiting for transfers between devices, local(): lax.all_to_all(queries, 'seq', split_axis=2, concat_axis=1, tiled=True)  43.1 us
    all_to_all x1, waiting for transfers between devices, local(): lax.all_to_all(enc_values, 'seq', split_axis=2, concat_axis=1, tiled=True)  42.1 us
    all_to_all x1, waiting for transfers between devices, local(): lax.all_to_all(enc_keys, 'seq', split_axis=2, concat_axis=1, tiled=True)  39.2 us
    reduce_sum x8, other arithmetic, attend_dense(): row_total = jnp.sum(expos, axis=2, keepdims=True)  27.4 us
    unnamed x7, local copies, waits for them, and re-layouts  27.3 us
  transfers between devices with their start and end apart: 5, of which 5 were waited for; matrix products, arithmetic and copies ran while one was open for 6% of the time, Pallas kernels for 0%

commit v1 on v0

--- a/solution.py
+++ b/solution.py
@@ -5,6 +5,18 @@
 
 HEAD_DIM = 64
 masked_score = -1e30
+
+
+def rotated_exchange(value, axis, split, join):
+    ways, here = (lax.axis_size(axis), lax.axis_index(axis))
+    width = value.shape[split] // ways
+    turned = jnp.roll(value, -here * width, axis=split)
+    got = [lax.slice_in_dim(turned, 0, width, axis=split)]
+    for far in range(1, ways):
+        sent = lax.slice_in_dim(turned, far * width, (far + 1) * width, axis=split)
+        got.append(lax.ppermute(sent, axis, [(d, (d + far) % ways) for d in range(ways)]))
+    line = jnp.concatenate(got[::-1], axis=join)
+    return jnp.roll(line, (here + 1) * got[0].shape[join], axis=join)
 
 
 def shortened(value):
@@ -53,7 +65,7 @@
     members = (
         lax.all_to_all(queries, "seq", split_axis=2, concat_axis=1, tiled=True),
         lax.all_to_all(enc_keys, "seq", split_axis=2, concat_axis=1, tiled=True),
-        lax.all_to_all(enc_values, "seq", split_axis=2, concat_axis=1, tiled=True),
+        rotated_exchange(enc_values, "seq", 2, 1),
         lax.all_to_all(dec_spread, "seq", split_axis=2, concat_axis=1, tiled=True),
         lax.all_to_all(enc_spread, "seq", split_axis=2, concat_axis=1, tiled=True),
     )

time: 415 us -> 464 us (1.12)
  starting transfers between devices: 23.1 us -> 76.9 us
  waiting for transfers between devices: 133 us -> 123 us
    ppermute x0 -> x7, waiting for transfers between devices: none -> 72.3 us  [rotated_exchange(): lax.ppermute(sent, axis, [(d, (d + far) % ways) for d in range(ways)])]
    ppermute x0 -> x7, starting transfers between devices: none -> 58.1 us  [rotated_exchange(): lax.ppermute(sent, axis, [(d, (d + far) % ways) for d in range(ways)])]
    all_to_all x1 -> x0, waiting for transfers between devices: 42.1 us -> none  [local(): lax.all_to_all(enc_values, 'seq', split_axis=2, concat_axis=1, tiled=True)]
    all_to_all x1, waiting for transfers between devices: 39.2 us -> 0.01 us  [local(): lax.all_to_all(enc_keys, 'seq', split_axis=2, concat_axis=1, tiled=True)]
    while x4 -> x3, local copies, waits for them, and re-layouts: 17.8 us -> 12.9 us  [local(): lax.map(one_row, (query_rows, key_rows, value_rows, dec_rows, enc_rows))]
    unnamed x7 -> x25, local copies, waits for them, and re-layouts: 27.3 us -> 30.2 us
  transfers between devices with their start and end apart: 5 -> 11, of which waited for: 5 -> 6; matrix products, arithmetic and copies ran while one was open for 6% -> 6% of each run, Pallas kernels for 0% -> 0%
where the time goes in v1:
time: 464 us; the launch traced here: 462 us
  waiting for transfers between devices  123 us (27%)
  matrix products  122 us (26%)
  starting transfers between devices  76.9 us (17%)
  local copies, waits for them, and re-layouts  56.8 us (12%)
  blocking collectives  50.8 us (11%)
  other arithmetic  32.4 us (7%)
    dot_general x32, matrix products, attend_dense(): jnp.einsum('qhd,khd->hqk', query_heads[offset:offset + query_span], key_h...  75.8 us
    ppermute x7, waiting for transfers between devices, rotated_exchange(): lax.ppermute(sent, axis, [(d, (d + far) % ways) for d in range(ways)])  72.3 us
    ppermute x7, starting transfers between devices, rotated_exchange(): lax.ppermute(sent, axis, [(d, (d + far) % ways) for d in range(ways)])  58.1 us
    all_to_all x1, blocking collectives, local(): lax.all_to_all(shortened(attended), 'seq', split_axis=1, concat_axis=2, t...  50.8 us
    dot_general x32, matrix products, attend_dense(): jnp.einsum('hqk,khd->qhd', weights, value_heads, preferred_element_type=j...  45.8 us
    all_to_all x1, waiting for transfers between devices, local(): lax.all_to_all(queries, 'seq', split_axis=2, concat_axis=1, tiled=True)  42.1 us
    unnamed x25, local copies, waits for them, and re-layouts  30.2 us
    reduce_sum x8, other arithmetic, attend_dense(): row_total = jnp.sum(expos, axis=2, keepdims=True)  27.4 us
  transfers between devices with their start and end apart: 11, of which 6 were waited for; matrix products, arithmetic and copies ran while one was open for 6% of the time, Pallas kernels for 0%

profile of v1, /device:TPU:0, one launch (start us, length us, event | category | flops | bytes accessed | tf_op | source)
XLA Modules:
  0.0 461.8 jit_solution(1685660452593663048)
XLA Ops:
  1.3 7.3 %all-to-all-start = ((bf16[8,256,8]{1,0,2:T(8,128)(2,1)}), bf16[8,256,8]{1,0,2:T(8,128)(2,1)S(1)}, u32[]{:S(2)}, u32[]{:S(2)}) async-start(bf16[8,256,8]{1,0,2:T(8,128)(2,1)} %broadcast_in_dim.23), calls=%async_computation | async-start | bytes 65536 | tf_op jit(solution)/shard_map/all_to_all | solution.py:69
  9.3 6.0 %all-to-all-done = bf16[8,256,8]{1,0,2:T(8,128)(2,1)S(1)} async-done(((bf16[8,256,8]{1,0,2:T(8,128)(2,1)}), bf16[8,256,8]{1,0,2:T(8,128)(2,1)S(1)}, u32[]{:S(2)}, u32[]{:S(2)}) %all-to-all-start) | async-done | bytes 32800 | tf_op jit(solution)/shard_map/all_to_all | solution.py:69
  19.2 4.5 copy.20
  25.8 3.8 all-to-all-start.2
  29.7 4.5 copy.23
  34.2 42.1 %all-to-all-done.2 = bf16[8,256,512]{1,0,2:T(8,128)(2,1)S(1)} async-done(((bf16[8,256,512]{1,0,2:T(8,128)(2,1)}), bf16[8,256,512]{1,0,2:T(8,128)(2,1)S(1)}, u32[]{:S(2)}, u32[]{:S(2)}) %all-to-all-start.2) | async-done | bytes 2097184 | tf_op jit(solution)/shard_map/all_to_all | solution.py:66
  76.3 4.4 all-to-all-start.3
  86.6 4.8 %collective-permute-start = (bf16[8,256,64]{2,1,0:T(8,128)(2,1)}, bf16[8,256,64]{2,1,0:T(8,128)(2,1)S(1)}, u32[]{:S(2)}, u32[]{:S(2)}) collective-permute-start(bf16[8,256,64]{2,1,0:T(8,128)(2,1)} %get-tuple-element.91), channel_id=1, source_target_pairs={{0,7},{1,0},{2,1},{3,2},{4,3},{5,4},{6,5},{7,6},{8,15},{9,8},{10,9... | collective-permute-start | bytes 786440 | tf_op jit(solution)/shard_map/ppermute | solution.py:17
  94.9 32.6 %collective-permute-done = bf16[8,256,64]{2,1,0:T(8,128)(2,1)S(1)} collective-permute-done((bf16[8,256,64]{2,1,0:T(8,128)(2,1)}, bf16[8,256,64]{2,1,0:T(8,128)(2,1)S(1)}, u32[]{:S(2)}, u32[]{:S(2)}) %collective-permute-start) | collective-permute-done | bytes 262176 | tf_op jit(solution)/shard_map/ppermute | solution.py:17
  127.5 11.2 %collective-permute-done.1 = bf16[8,256,64]{2,1,0:T(8,128)(2,1)S(1)} collective-permute-done((bf16[8,256,64]{2,1,0:T(8,128)(2,1)}, bf16[8,256,64]{2,1,0:T(8,128)(2,1)S(1)}, u32[]{:S(2)}, u32[]{:S(2)}) %collective-permute-start.1) | collective-permute-done | bytes 262176 | tf_op jit(solution)/shard_map/ppermute | solution.py:17
  138.7 49.8 %collective-permute-start.6 = (bf16[8,256,64]{2,1,0:T(8,128)(2,1)}, bf16[8,256,64]{2,1,0:T(8,128)(2,1)S(1)}, u32[]{:S(2)}, u32[]{:S(2)}) collective-permute-start(bf16[8,256,64]{2,1,0:T(8,128)(2,1)} %get-tuple-element.85), channel_id=1, source_target_pairs={{0,1},{1,2},{2,3},{3,4},{4,5},{5,6},{6,7},{7,0},{8,9},{9,10},{10,1... | collective-permute-start | bytes 786440 | tf_op jit(solution)/shard_map/ppermute | solution.py:17
  189.7 28.6 %collective-permute-done.3 = bf16[8,256,64]{2,1,0:T(8,128)(2,1)} collective-permute-done((bf16[8,256,64]{2,1,0:T(8,128)(2,1)}, bf16[8,256,64]{2,1,0:T(8,128)(2,1)}, u32[]{:S(2)}, u32[]{:S(2)}) %collective-permute-start.3) | collective-permute-done | bytes 262176 | tf_op jit(solution)/shard_map/ppermute | solution.py:17
  227.0 3.5 copy.33
  230.4 5.1 %copy.35 = bf16[8,8,256,64]{3,2,1,0:T(8,128)(2,1)} copy(bf16[8,8,256,64]{2,0,3,1:T(8,128)(2,1)} %bitcast.36) | data formatting | bytes 4194304 | tf_op jit(solution)/shard_map/while | solution.py:82
  235.6 150.6 %while.10 = (s32[]{:T(128)}, bf16[8,2048,64]{1,2,0:T(8,128)(2,1)S(1)}, bf16[8,2048,64]{2,1,0:T(8,128)(2,1)}, s32[8,2048]{1,0:T(8,128)S(1)}, s32[8,2048]{1,0:T(8,...) while((s32[]{:T(128)}, ...), condition=%wide.region_9.10_spmd, body=%wide.region_0.9_spmd.sunk | while | flops 1133637632 | bytes 72773864 | solution.py:82
  241.3 3.9 fusion.87
  260.1 3.9 fusion.87
  265.5 3.4 fusion.88
  279.0 3.9 fusion.87
  284.3 3.4 fusion.88
  297.8 3.9 fusion.87
  316.6 3.9 fusion.87
  321.9 3.4 fusion.88
  335.5 3.9 fusion.87
  340.8 3.4 fusion.88
  354.3 3.9 fusion.87
  373.1 3.9 fusion.87
  386.2 4.3 copy.28
  390.5 6.4 %reshape.166 = bf16[8,2,65536]{2,1,0:T(2,128)(2,1)S(1)} reshape(bf16[2048,8,64]{2,1,0:T(8,128)(2,1)} %bitcast.143) | data formatting | bytes 4194304
  396.9 50.8 %all_to_all.72 = bf16[8,2,65536]{2,1,0:T(2,128)(2,1)} all-to-all(bf16[8,2,65536]{2,1,0:T(2,128)(2,1)S(1)} %reshape.166), channel_id=1, replica_groups=mesh['dp'=4,'seq'=8] {'seq'}, dimensions={0} | all-to-all | bytes 4194304 | tf_op jit(solution)/shard_map/all_to_all | solution.py:83
  447.6 7.4 %reshape.167 = bf16[2048,8,64]{2,1,0:T(8,128)(2,1)} reshape(bf16[8,2,65536]{2,1,0:T(2,128)(2,1)} %all_to_all.72) | data formatting | bytes 4194304
  455.0 4.5 copy.30
  (145 shorter events, 135.0 us)
Async XLA Ops:
  1.3 14.0 %all-to-all-start = ((bf16[8,256,8]{1,0,2:T(8,128)(2,1)}), bf16[8,256,8]{1,0,2:T(8,128)(2,1)S(1)}, u32[]{:S(2)}, u32[]{:S(2)}) async-start(bf16[8,256,8]{1,0,2:T(8,128)(2,1)} %broadcast_in_dim.23), calls=%async_computation | async-start | bytes 65536 | tf_op jit(solution)/shard_map/all_to_all | solution.py:69
  15.9 10.0 %all-to-all-start.1 = ((bf16[8,256,8]{1,0,2:T(8,128)(2,1)}), bf16[8,256,8]{1,0,2:T(8,128)(2,1)S(1)}, u32[]{:S(2)}, u32[]{:S(2)}) async-start(bf16[8,256,8]{1,0,2:T(8,128)(2,1)} %broadcast_in_dim.24), calls=%async_computation.1 | async-start | bytes 65536 | tf_op jit(solution)/shard_map/all_to_all | solution.py:70
  25.8 50.4 %all-to-all-start.2 = ((bf16[8,256,512]{1,0,2:T(8,128)(2,1)}), bf16[8,256,512]{1,0,2:T(8,128)(2,1)S(1)}, u32[]{:S(2)}, u32[]{:S(2)}) async-start(bf16[8,256,512]{1,0,2:T(8,128)(2,1)} %copy.20), calls=%async_computation.2 | async-start | bytes 4194304 | tf_op jit(solution)/shard_map/all_to_all | solution.py:66
  76.3 4.4 copy-start
  76.3 154.1 %all-to-all-start.3 = ((bf16[8,256,512]{1,0,2:T(8,128)(2,1)}), bf16[8,256,512]{1,0,2:T(8,128)(2,1)}, u32[]{:S(2)}, u32[]{:S(2)}) async-start(bf16[8,256,512]{1,0,2:T(8,128)(2,1)} %copy.23), calls=%async_computation.3 | async-start | bytes 4194304 | tf_op jit(solution)/shard_map/all_to_all | solution.py:67
  86.6 40.9 %collective-permute-start = (bf16[8,256,64]{2,1,0:T(8,128)(2,1)}, bf16[8,256,64]{2,1,0:T(8,128)(2,1)S(1)}, u32[]{:S(2)}, u32[]{:S(2)}) collective-permute-start(bf16[8,256,64]{2,1,0:T(8,128)(2,1)} %get-tuple-element.91), channel_id=1, source_target_pairs={{0,7},{1,0},{2,1},{3,2},{4,3},{5,4},{6,5},{7,6},{8,15},{9,8},{10,9... | collective-permute-start | bytes 786440 | tf_op jit(solution)/shard_map/ppermute | solution.py:17
  91.4 47.3 %collective-permute-start.1 = (bf16[8,256,64]{2,1,0:T(8,128)(2,1)}, bf16[8,256,64]{2,1,0:T(8,128)(2,1)S(1)}, u32[]{:S(2)}, u32[]{:S(2)}) collective-permute-start(bf16[8,256,64]{2,1,0:T(8,128)(2,1)} %get-tuple-element.90), channel_id=1, source_target_pairs={{0,6},{1,7},{2,0},{3,1},{4,2},{5,3},{6,4},{7,5},{8,14},{9,15},{10,... | collective-permute-start | bytes 786440 | tf_op jit(solution)/shard_map/ppermute | solution.py:17
  91.9 96.7 %collective-permute-start.2 = (bf16[8,256,64]{2,1,0:T(8,128)(2,1)}, bf16[8,256,64]{2,1,0:T(8,128)(2,1)}, u32[]{:S(2)}, u32[]{:S(2)}) collective-permute-start(bf16[8,256,64]{2,1,0:T(8,128)(2,1)} %get-tuple-element.89), channel_id=1, source_target_pairs={{0,5},{1,6},{2,7},{3,0},{4,1},{5,2},{6,3},{7,4},{8,13},{9,14},{10,... | collective-permute-start | bytes 786440 | tf_op jit(solution)/shard_map/ppermute | solution.py:17
  91.9 126.4 %collective-permute-start.3 = (bf16[8,256,64]{2,1,0:T(8,128)(2,1)}, bf16[8,256,64]{2,1,0:T(8,128)(2,1)}, u32[]{:S(2)}, u32[]{:S(2)}) collective-permute-start(bf16[8,256,64]{2,1,0:T(8,128)(2,1)} %get-tuple-element.88), channel_id=1, source_target_pairs={{0,4},{1,5},{2,6},{3,7},{4,0},{5,1},{6,2},{7,3},{8,12},{9,13},{10,... | collective-permute-start | bytes 786440 | tf_op jit(solution)/shard_map/ppermute | solution.py:17
  94.8 124.6 %collective-permute-start.4 = (bf16[8,256,64]{2,1,0:T(8,128)(2,1)}, bf16[8,256,64]{2,1,0:T(8,128)(2,1)}, u32[]{:S(2)}, u32[]{:S(2)}) collective-permute-start(bf16[8,256,64]{2,1,0:T(8,128)(2,1)} %get-tuple-element.87), channel_id=1, source_target_pairs={{0,3},{1,4},{2,5},{3,6},{4,7},{5,0},{6,1},{7,2},{8,11},{9,12},{10,... | collective-permute-start | bytes 786440 | tf_op jit(solution)/shard_map/ppermute | solution.py:17
  127.4 93.1 %collective-permute-start.5 = (bf16[8,256,64]{2,1,0:T(8,128)(2,1)}, bf16[8,256,64]{2,1,0:T(8,128)(2,1)S(1)}, u32[]{:S(2)}, u32[]{:S(2)}) collective-permute-start(bf16[8,256,64]{2,1,0:T(8,128)(2,1)} %get-tuple-element.86), channel_id=1, source_target_pairs={{0,2},{1,3},{2,4},{3,5},{4,6},{5,7},{6,0},{7,1},{8,10},{9,11},{10,... | collective-permute-start | bytes 786440 | tf_op jit(solution)/shard_map/ppermute | solution.py:17
  138.7 81.9 %collective-permute-start.6 = (bf16[8,256,64]{2,1,0:T(8,128)(2,1)}, bf16[8,256,64]{2,1,0:T(8,128)(2,1)S(1)}, u32[]{:S(2)}, u32[]{:S(2)}) collective-permute-start(bf16[8,256,64]{2,1,0:T(8,128)(2,1)} %get-tuple-element.85), channel_id=1, source_target_pairs={{0,1},{1,2},{2,3},{3,4},{4,5},{5,6},{6,7},{7,0},{8,9},{9,10},{10,1... | collective-permute-start | bytes 786440 | tf_op jit(solution)/shard_map/ppermute | solution.py:17
  224.6 2.3 copy-start.1
  230.4 5.1 %copy-start.3 = (bf16[8,2048,64]{1,2,0:T(8,128)(2,1)S(1)}, bf16[8,2048,64]{1,2,0:T(8,128)(2,1)}, u32[]{:S(2)}) copy-start(bf16[8,2048,64]{1,2,0:T(8,128)(2,1)} %custom-call.1) | copy-start | bytes 6291460
  241.3 3.9 copy-start.2
  260.1 3.9 copy-start.2
  279.0 3.9 copy-start.2
  297.8 3.9 copy-start.2
  316.6 3.9 copy-start.2
  335.4 3.9 copy-start.2
  354.3 3.9 copy-start.2
  373.1 3.9 copy-start.2
